TPU v7x, 32 devices: a whole 2x2x4 slice. The times are simulated.
32 devices in a mesh: row: 8 (over y, x, core), col: 4 (over z).
Axes of the slice: x: 2, y: 2, z: 4, core: 2. Of those that a mesh axis runs over, the one named last changes fastest.
Arguments:
- alignment_state: bfloat16 [128, 128, 256], P('col', 'row'), may hold values from -6 to 6
- layer_norm_gain: float32 [256], replicated, may hold values from 0.1 to 1.9
- left_weight_matrix: bfloat16 [256, 32], replicated, may hold values from -0.375 to 0.375
- right_weight_matrix: bfloat16 [256, 32], replicated, may hold values from -0.375 to 0.375
- output_weight_matrix: bfloat16 [1024, 128], replicated, may hold values from -0.1875 to 0.1875
- output_bias_vector: float32 [128], replicated, may hold values from -3 to 3
- pair_update_cotangent: bfloat16 [128, 128, 128], P('row', 'col'), may hold values from -40 to 40
Outputs:
- pair_update_output: bfloat16 [128, 128, 128], P('row', 'col')
- alignment_gradient: bfloat16 [128, 128, 256], P('col', 'row')
- left_weight_gradient: float32 [256, 32], replicated
- right_weight_gradient: float32 [256, 32], replicated
- out_w_grad: float32 [1024, 128], P(('row', 'col'))
- norm_gain_gradient: float32 [256], replicated
- output_bias_gradient: float32 [128], replicated
All inputs are finite; a program needn't handle non-finite values.
Results may differ from a plain program's by a relative error of at most 0.024.
Values may be sent and summed in bfloat16 or wider, within the bound.
No kernel may reach another device: no remote copies, remote signals or barrier semaphores. Data moves between devices by JAX's collectives and lax.ppermute only.
A program may use at most 64 MiB of HBM per device.

v0:
```python
import jax
import jax.numpy as jnp
from jax import lax
from jax.sharding import PartitionSpec as P


def from_root(block, axis, holder):
    block = jnp.where(lax.axis_index(axis) == holder, block, jnp.zeros_like(block))
    return lax.psum(block, axis)


def apply_layer_norm(alignment_state):
    value_entries = alignment_state.astype(jnp.float32)
    center = value_entries - jnp.mean(value_entries, axis=-1, keepdims=True)
    inverse_deviation = lax.rsqrt(jnp.mean(center * center, axis=-1, keepdims=True) + 1e-05)
    return (center * inverse_deviation, inverse_deviation)


def on_device(
    alignment_state,
    layer_norm_gain,
    left_weight_matrix,
    right_weight_matrix,
    output_weight_matrix,
    output_bias_vector,
    pair_update_cotangent,
):
    sequence_block_local, residue_block_local, alignment_weight = alignment_state.shape
    proj_w = left_weight_matrix.shape[1]
    pair_w = output_weight_matrix.shape[1]
    row_count = lax.axis_size("row")
    col_count = lax.axis_size("col")
    row_ratio = row_count // col_count
    total_res = residue_block_local * row_count
    col_res = residue_block_local * row_ratio
    col_index = lax.axis_index("col")
    row_index = lax.axis_index("row")
    normed_alignment, inverse_deviation = apply_layer_norm(alignment_state)
    layer_norm_output = (normed_alignment * layer_norm_gain).astype(jnp.bfloat16)
    normed_flat_rows = layer_norm_output.reshape(-1, alignment_weight)
    left_local = (
        jnp.dot(normed_flat_rows, left_weight_matrix, preferred_element_type=jnp.float32)
        .astype(jnp.bfloat16)
        .reshape(sequence_block_local, residue_block_local, proj_w)
    )
    right_local = (
        jnp.dot(normed_flat_rows, right_weight_matrix, preferred_element_type=jnp.float32)
        .astype(jnp.bfloat16)
        .reshape(sequence_block_local, residue_block_local, proj_w)
    )
    left_all, right_rows = (
        lax.all_gather(left_local, "col", axis=0, tiled=True),
        lax.all_gather(right_local, "col", axis=0, tiled=True),
    )
    seq_total = left_all.shape[0]
    right_every = lax.all_gather(right_rows, "row", axis=1, tiled=True)
    right_block = lax.dynamic_slice_in_dim(right_every, col_index * col_res, col_res, 1)
    block_res = min(8, residue_block_local)

    def visit(totals, row_start):
        right_acc, projection_running_sum = totals
        left_part = lax.dynamic_slice_in_dim(left_all, row_start, block_res, 1)
        cot_part = lax.dynamic_slice_in_dim(pair_update_cotangent, row_start, block_res, 0)
        outer_prod = jnp.einsum(
            "sic,sjd->ijcd", left_part, right_block, preferred_element_type=jnp.float32
        )
        outer_flat = (
            (outer_prod / seq_total)
            .astype(jnp.bfloat16)
            .reshape(block_res * col_res, proj_w * proj_w)
        )
        cot_flat = cot_part.reshape(block_res * col_res, pair_w)
        pair_part = (
            jnp.dot(outer_flat, output_weight_matrix, preferred_element_type=jnp.float32)
            + output_bias_vector
        ).astype(jnp.bfloat16)
        projection_running_sum = projection_running_sum + lax.dot_general(
            outer_flat, cot_flat, (((0,), (0,)), ((), ())), preferred_element_type=jnp.float32
        )
        outer_grad = lax.dot_general(
            cot_flat,
            output_weight_matrix,
            (((1,), (1,)), ((), ())),
            preferred_element_type=jnp.float32,
        ).astype(jnp.bfloat16)
        outer_grad = outer_grad.reshape(block_res, col_res, proj_w, proj_w)
        left_part_grad = (
            jnp.einsum("ijcd,sjd->sic", outer_grad, right_block, preferred_element_type=jnp.float32)
            / seq_total
        )
        right_acc = (
            right_acc
            + jnp.einsum("ijcd,sic->sjd", outer_grad, left_part, preferred_element_type=jnp.float32)
            / seq_total
        )
        return (
            (right_acc, projection_running_sum),
            (pair_part.reshape(block_res, col_res, pair_w), left_part_grad),
        )

    starts = jnp.arange(residue_block_local // block_res, dtype=jnp.int32) * block_res
    initial = (
        jnp.zeros((seq_total, col_res, proj_w), jnp.float32),
        jnp.zeros((proj_w * proj_w, pair_w), jnp.float32),
    )
    (right_acc, projection_running_sum), (pair_parts, left_parts) = lax.scan(visit, initial, starts)
    pair_update_output = pair_parts.reshape(residue_block_local, col_res, pair_w)
    left_partial = jnp.transpose(left_parts, (1, 0, 2, 3)).reshape(
        seq_total, residue_block_local, proj_w
    )
    left_d = lax.psum_scatter(
        left_partial.astype(jnp.bfloat16), "col", scatter_dimension=0, tiled=True
    )
    right_full = lax.psum(right_acc.astype(jnp.bfloat16), "row").astype(jnp.float32)
    right_half = lax.dynamic_slice_in_dim(
        right_full, row_index % row_ratio * residue_block_local, residue_block_local, 1
    )
    right_home = from_root(right_half.astype(jnp.bfloat16), "col", row_index // row_ratio).astype(
        right_half.dtype
    )
    right_d = lax.dynamic_slice_in_dim(
        right_home, col_index * sequence_block_local, sequence_block_local, 0
    ).astype(jnp.bfloat16)
    left_flat = left_d.reshape(-1, proj_w)
    right_flat = right_d.reshape(-1, proj_w)
    normed_derivative = lax.dot_general(
        left_flat, left_weight_matrix, (((1,), (1,)), ((), ())), preferred_element_type=jnp.float32
    )
    normed_derivative = normed_derivative + lax.dot_general(
        right_flat,
        right_weight_matrix,
        (((1,), (1,)), ((), ())),
        preferred_element_type=jnp.float32,
    )
    normed_derivative = normed_derivative.reshape(
        sequence_block_local, residue_block_local, alignment_weight
    )
    scaled_product = normed_derivative * layer_norm_gain
    alignment_gradient = (
        (
            scaled_product
            - jnp.mean(scaled_product, axis=-1, keepdims=True)
            - normed_alignment * jnp.mean(scaled_product * normed_alignment, axis=-1, keepdims=True)
        )
        * inverse_deviation
    ).astype(jnp.bfloat16)
    weight_left = lax.dot_general(
        normed_flat_rows, left_flat, (((0,), (0,)), ((), ())), preferred_element_type=jnp.float32
    )
    weight_right = lax.dot_general(
        normed_flat_rows, right_flat, (((0,), (0,)), ((), ())), preferred_element_type=jnp.float32
    )
    gain_part = jnp.sum(normed_derivative * normed_alignment, axis=(0, 1))
    bias_part = jnp.sum(pair_update_cotangent, axis=(0, 1), dtype=jnp.float32)
    param_totals = lax.psum((weight_left, weight_right, gain_part, bias_part), ("row", "col"))
    proj_partial = lax.psum_scatter(
        projection_running_sum.astype(jnp.bfloat16), "row", scatter_dimension=0, tiled=True
    ).astype(jnp.float32)
    proj_total = lax.psum_scatter(proj_partial, "col", scatter_dimension=0, tiled=True)
    return (
        pair_update_output,
        alignment_gradient,
        param_totals[0] / total_res,
        param_totals[1] / total_res,
        proj_total / total_res,
        param_totals[2] / total_res,
        param_totals[3] / total_res,
    )


def solution(mesh):
    return jax.shard_map(
        on_device,
        mesh=mesh,
        in_specs=(P("col", "row", None), P(), P(), P(), P(), P(), P("row", "col", None)),
        out_specs=(
            P("row", "col", None),
            P("col", "row", None),
            P(),
            P(),
            P(("row", "col"), None),
            P(),
            P(),
        ),
        check_vma=False,
    )
```

profile of v0, /device:TPU:0, one launch (start us, length us, event | category | flops | bytes accessed | tf_op | source)
XLA Modules:
  0.0 416.1 jit_solution(7871246451103388164)
XLA Ops:
  11.1 18.0 %all_gather.10 = bf16[128,16,32]{2,1,0:T(8,128)(2,1)} all-gather(bf16[32,16,32]{2,1,0:T(8,128)(2,1)S(1)} %bitcast.126), channel_id=1, replica_groups=mesh['row'=8,'col'=4] {'col'}, dimensions={0}, use_global_device_ids=true | all-gather | bytes 163840 | tf_op jit(solution)/shard_map/all_gather | solution.py:53
  29.6 16.3 %all_gather.9 = bf16[128,16,32]{2,1,0:T(8,128)(2,1)S(1)} all-gather(bf16[32,16,32]{2,1,0:T(8,128)(2,1)S(1)} %bitcast.127), channel_id=1, replica_groups=mesh['row'=8,'col'=4] {'col'}, dimensions={0}, use_global_device_ids=true | all-gather | bytes 163840 | tf_op jit(solution)/shard_map/all_gather | solution.py:52
  46.8 21.7 %all-gather.2.cloned.1.call-done = bf16[128,128,32]{2,1,0:T(8,128)(2,1)} async-done(((bf16[128,16,32]{2,1,0:T(8,128)(2,1)}), bf16[128,128,32]{2,1,0:T(8,128)(2,1)}) %all-gather.2.cloned.1.call-update) | async-done | bytes 1048592 | tf_op jit(solution)/shard_map/all_gather | solution.py:56
  69.8 1.8 copy.44
  71.6 32.6 %while.17 = (s32[]{:T(128)}, f32[128,32,32]{0,2,1:T(8,128)}, f32[1024,128]{1,0:T(8,128)S(1)}, bf16[2,8,32,128]{3,2,1,0:T(8,128)(2,1)}, bf16[2,128,8,32]{1,3,2,0:...) while((s32[]{:T(128)}, f32[128,32,32]{0,2,1:T(8,128)}, ...), condition=%wide.region_3.4_spmd.clone, body=%wide.region_2.3_spmd.clone.sunk | while | flops 404193280 | bytes 15928666 | solution.py:106
  74.8 1.7 fusion.79
  76.5 2.2 reshape.95
  81.1 1.6 reshape.94
  85.3 2.1 fusion.81
  90.6 1.7 fusion.79
  92.2 2.2 reshape.95
  96.9 1.6 reshape.94
  98.5 2.6 fusion.78
  102.1 2.1 fusion.81
  104.3 1.8 convert_element_type.67
  106.2 2.1 copy.45
  109.0 51.2 %all-reduce.5.cloned.1.call-done = bf16[128,32,32]{0,2,1:T(8,128)(2,1)} async-done(((bf16[128,32,32]{0,2,1:T(8,128)(2,1)}), bf16[128,32,32]{0,2,1:T(8,128)(2,1)}) %all-reduce.5.cloned.1.call-update) | async-done | bytes 262160 | tf_op jit(solution)/shard_map/psum | solution.py:114
  160.2 1.6 fusion.28
  161.8 21.9 %reduce-scatter.4.cloned.1.call-done = bf16[32,16,32]{2,1,0:T(8,128)(2,1)} async-done(((bf16[128,16,32]{2,1,0:T(8,128)(2,1)}), bf16[32,16,32]{2,1,0:T(8,128)(2,1)}) %reduce-scatter.4.cloned.1.call-update) | async-done | bytes 32784 | tf_op jit(solution)/shard_map/reduce_scatter | solution.py:111
  184.8 1.7 convolution_bitcast_fusion.3
  186.5 32.9 %all-reduce.7.cloned.1.call-done = bf16[128,16,32]{0,2,1:T(8,128)(2,1)} async-done(((bf16[128,16,32]{0,2,1:T(8,128)(2,1)}), bf16[128,16,32]{0,2,1:T(8,128)(2,1)}) %all-reduce.7.cloned.1.call-update) | async-done | bytes 131088 | tf_op jit(solution)/shard_map/psum | solution.py:9
  224.5 122.1 %all-reduce.9.cloned.1.call-done = (f32[256,32]{0,1:T(8,128)}, f32[256,32]{0,1:T(8,128)}, f32[256]{0:T(256)}, f32[128]{0:T(128)}) async-done(((f32[256,32]{0,1:T(8,128)}, f32[256,32]{0,1:T(8,128)}, f32[256]{0:T(256)}, f32[128]{0:T(128)}), (f32[256,32]{0,1:T(8,128)}, f32[256,32]{0,1:T(8,128)}, f32[256]{0:T(256)}, f32[128]{0:T(128)})) %all-reduce.9.cloned.1.call-update) | async-done | bytes 67088 | tf_op jit(solution)/shard_map/psum | solution.py:155
  349.3 37.1 %reduce-scatter.6.cloned.1.call-done = bf16[128,128]{1,0:T(8,128)(2,1)} async-done(((bf16[1024,128]{1,0:T(8,128)(2,1)}), bf16[128,128]{1,0:T(8,128)(2,1)}) %reduce-scatter.6.cloned.1.call-update) | async-done | bytes 32784 | tf_op jit(solution)/shard_map/reduce_scatter | solution.py:156
  388.9 19.1 %reduce-scatter.8.cloned.1.call-done = f32[32,128]{1,0:T(8,128)} async-done(((f32[128,128]{1,0:T(8,128)}), f32[32,128]{1,0:T(8,128)}) %reduce-scatter.8.cloned.1.call-update) | async-done | bytes 16400 | tf_op jit(solution)/shard_map/reduce_scatter | solution.py:159
  (106 shorter events, 30.6 us)
Async XLA Ops:
  7.2 3.6 copy-start
  7.2 22.1 %copy-start.12 = (bf16[256,32]{0,1:T(8,128)(2,1)S(1)}, bf16[256,32]{0,1:T(8,128)(2,1)}, u32[]{:S(2)}) copy-start(bf16[256,32]{0,1:T(8,128)(2,1)} %param.11) | copy-start | bytes 49156
  7.2 61.3 %all-gather.2.cloned.1.call-start = ((), (), s32[]{:S(2)}) async-start(), calls=%async_computation.3 | async-start | bytes 4718592 | tf_op jit(solution)/shard_map/all_gather | solution.py:56
  8.3 2.4 copy-start.8
  10.8 18.8 %copy-start.5 = (bf16[32,16,256]{2,1,0:T(8,128)(2,1)}, bf16[32,16,256]{2,1,0:T(8,128)(2,1)S(1)}, u32[]{:S(2)}) copy-start(bf16[32,16,256]{2,1,0:T(8,128)(2,1)S(1)} %fusion.21) | copy-start | bytes 786436
  29.1 131.0 %all-reduce.5.cloned.1.call-start = ((), (), s32[]{:S(2)}) async-start(), calls=%async_computation.5 | async-start | bytes 524288 | tf_op jit(solution)/shard_map/psum | solution.py:114
  45.9 25.7 %copy-start.1 = (bf16[1024,128]{1,0:T(8,128)(2,1)S(1)}, bf16[1024,128]{1,0:T(8,128)(2,1)}, u32[]{:S(2)}) copy-start(bf16[1024,128]{1,0:T(8,128)(2,1)} %param.13) | copy-start | bytes 786436
  82.7 1.9 copy-start.16
  84.3 3.1 copy-start.3
  98.5 2.7 copy-start.15
  98.5 2.9 copy-start.16
  101.1 3.1 copy-start.3
  104.2 4.1 copy-start.7
  104.2 79.5 %copy-start.13 = (bf16[256,32]{0,1:T(8,128)(2,1)S(1)}, bf16[256,32]{0,1:T(8,128)(2,1)}, u32[]{:S(2)}) copy-start(bf16[256,32]{0,1:T(8,128)(2,1)} %param.11) | copy-start | bytes 49156
  104.2 80.6 %copy-start.6 = (bf16[32,16,256]{2,1,0:T(8,128)(2,1)S(1)}, bf16[32,16,256]{2,1,0:T(8,128)(2,1)}, u32[]{:S(2)}) copy-start(bf16[32,16,256]{2,1,0:T(8,128)(2,1)} %copy-done.5) | copy-start | bytes 786436
  106.1 115.3 %copy-start.14 = (f32[256]{0:T(256)S(1)}, f32[256]{0:T(256)}, u32[]{:S(2)}) copy-start(f32[256]{0:T(256)} %param.10) | copy-start | bytes 3076
  106.1 77.6 %reduce-scatter.4.cloned.1.call-start = ((), (), s32[]{:S(2)}) async-start(), calls=%async_computation.4 | async-start | bytes 655360 | tf_op jit(solution)/shard_map/reduce_scatter | solution.py:111
  108.3 113.5 %copy-start.4 = (bf16[32,16,256]{2,1,0:T(8,128)(2,1)S(1)}, bf16[32,16,256]{2,1,0:T(8,128)(2,1)}, u32[]{:S(2)}) copy-start(bf16[32,16,256]{2,1,0:T(8,128)(2,1)} %param.9) | copy-start | bytes 786436
  108.3 113.5 %copy-start.9 = (f32[32,16]{1,0:T(8,128)S(1)}, f32[32,16]{1,0:T(8,128)}, u32[]{:S(2)}) copy-start(f32[32,16]{1,0:T(8,128)} %copy-done.8) | copy-start | bytes 6148
  108.3 113.5 %copy-start.11 = (f32[32,16]{1,0:T(8,128)S(1)}, f32[32,16]{1,0:T(8,128)}, u32[]{:S(2)}) copy-start(f32[32,16]{1,0:T(8,128)} %copy-done.10) | copy-start | bytes 6148
  108.3 111.1 %all-reduce.7.cloned.1.call-start = ((), (), s32[]{:S(2)}) async-start(), calls=%async_computation.6 | async-start | bytes 262144 | tf_op jit(solution)/shard_map/psum | solution.py:9
  161.8 184.9 %all-reduce.9.cloned.1.call-start = ((), (), s32[]{:S(2)}) async-start(), calls=%async_computation.9 | async-start | bytes 134144 | tf_op jit(solution)/shard_map/psum | solution.py:155
  222.5 163.9 %reduce-scatter.6.cloned.1.call-start = ((), (), s32[]{:S(2)}) async-start(), calls=%async_computation.7 | async-start | bytes 294912 | tf_op jit(solution)/shard_map/reduce_scatter | solution.py:156
  223.3 184.6 %reduce-scatter.8.cloned.1.call-start = ((), (), s32[]{:S(2)}) async-start(), calls=%async_computation.8 | async-start | bytes 81920 | tf_op jit(solution)/shard_map/reduce_scatter | solution.py:159
  (6 other events, 5.7 us)
Sparse Core Ops, SparseCore 0:
  29.3 39.2 all-gather.1
  106.2 53.8 all-reduce.4
  162.4 21.2 reduce-scatter.3
  186.5 32.8 all-reduce.6
  225.9 120.6 all-reduce.8
  349.5 36.8 reduce-scatter.5
  388.6 19.2 reduce-scatter.7
where the time goes:
time: 417 us; the launch traced here: 416 us
  waiting for transfers between devices  306 us (73%)
  blocking collectives  34.3 us (8%)
  local copies, waits for them, and re-layouts  21 us (5%)
  matrix products  18.1 us (4%)
  other arithmetic  18 us (4%)
  between operations  14.4 us (3%)
    psum x1, waiting for transfers between devices, on_device(): lax.psum((weight_left, weight_right, gain_part, bias_part), ('row', 'col'))  122 us
    psum x1, waiting for transfers between devices, on_device(): lax.psum(right_acc.astype(jnp.bfloat16), 'row').astype(jnp.float32)  51.2 us
    reduce_scatter x1, waiting for transfers between devices, on_device(): lax.psum_scatter(projection_running_sum.astype(jnp.bfloat16), 'row', scat...  37.1 us
    psum x1, waiting for transfers between devices, from_root(): return lax.psum(block, axis)  32.9 us
    reduce_scatter x1, waiting for transfers between devices, on_device(): lax.psum_scatter(left_partial.astype(jnp.bfloat16), 'col', scatter_dimens...  21.9 us
    all_gather x1, waiting for transfers between devices, on_device(): right_every = lax.all_gather(right_rows, 'row', axis=1, tiled=True)  21.7 us
    reduce_scatter x1, waiting for transfers between devices, on_device(): lax.psum_scatter(proj_partial, 'col', scatter_dimension=0, tiled=True)  19.1 us
    all_gather x1, blocking collectives, on_device(): lax.all_gather(right_local, 'col', axis=0, tiled=True)  18 us
  transfers between devices with their start and end apart: 7, of which 7 were waited for; matrix products, arithmetic and copies ran while one was open for 3% of the time, Pallas kernels for 0%

commit v1 on v0

--- a/solution.py
+++ b/solution.py
@@ -6,7 +6,7 @@
 
 def from_root(block, axis, holder):
     block = jnp.where(lax.axis_index(axis) == holder, block, jnp.zeros_like(block))
-    return lax.psum(block, axis)
+    return jnp.sum(lax.all_gather(block, axis), axis=0)
 
 
 def apply_layer_norm(alignment_state):

time: 417 us -> 382 us (0.916)
  waiting for transfers between devices: 306 us -> 252 us
  blocking collectives: 34.3 us -> 54.1 us
    psum x1 -> x0, waiting for transfers between devices: 32.9 us -> none  [from_root(): return lax.psum(block, axis)]
    all_gather x0 -> x1, blocking collectives: none -> 19.8 us  [from_root(): return jnp.sum(lax.all_gather(block, axis), axis=0)]
    reduce_scatter x1, waiting for transfers between devices: 21.9 us -> 2.88 us  [on_device(): lax.psum_scatter(left_partial.astype(jnp.bfloat16), 'col', scatter_dimens...]
  transfers between devices with their start and end apart: 7 -> 6, of which waited for: 7 -> 6; matrix products, arithmetic and copies ran while one was open for 3% -> 4% of each run, Pallas kernels for 0% -> 0%
where the time goes in v1:
time: 382 us; the launch traced here: 381 us
  waiting for transfers between devices  252 us (66%)
  blocking collectives  54.1 us (14%)
  local copies, waits for them, and re-layouts  21.1 us (6%)
  other arithmetic  18 us (5%)
  matrix products  17.3 us (5%)
  between operations  14.4 us (4%)
  loops' own time  4.07 us (1%)
    psum x1, waiting for transfers between devices, on_device(): lax.psum((weight_left, weight_right, gain_part, bias_part), ('row', 'col'))  121 us
    psum x1, waiting for transfers between devices, on_device(): lax.psum(right_acc.astype(jnp.bfloat16), 'row').astype(jnp.float32)  50.2 us
    reduce_scatter x1, waiting for transfers between devices, on_device(): lax.psum_scatter(projection_running_sum.astype(jnp.bfloat16), 'row', scat...  37.1 us
    all_gather x1, waiting for transfers between devices, on_device(): right_every = lax.all_gather(right_rows, 'row', axis=1, tiled=True)  21.7 us
    all_gather x1, blocking collectives, from_root(): return jnp.sum(lax.all_gather(block, axis), axis=0)  19.8 us
    reduce_scatter x1, waiting for transfers between devices, on_device(): lax.psum_scatter(proj_partial, 'col', scatter_dimension=0, tiled=True)  18.8 us
    all_gather x1, blocking collectives, on_device(): lax.all_gather(right_local, 'col', axis=0, tiled=True)  18 us
    all_gather x1, blocking collectives, on_device(): lax.all_gather(left_local, 'col', axis=0, tiled=True)  16.3 us
  transfers between devices with their start and end apart: 6, of which 6 were waited for; matrix products, arithmetic and copies ran while one was open for 4% of the time, Pallas kernels for 0%

profile of v1, /device:TPU:0, one launch (start us, length us, event | category | flops | bytes accessed | tf_op | source)
XLA Modules:
  0.0 381.0 jit_solution(3695146156068478806)
XLA Ops:
  11.1 18.0 %all_gather.16 = bf16[128,16,32]{2,1,0:T(8,128)(2,1)} all-gather(bf16[32,16,32]{2,1,0:T(8,128)(2,1)S(1)} %bitcast.128), channel_id=1, replica_groups=mesh['row'=8,'col'=4] {'col'}, dimensions={0}, use_global_device_ids=true | all-gather | bytes 163840 | tf_op jit(solution)/shard_map/all_gather | solution.py:53
  29.6 16.3 %all_gather.15 = bf16[128,16,32]{2,1,0:T(8,128)(2,1)S(1)} all-gather(bf16[32,16,32]{2,1,0:T(8,128)(2,1)S(1)} %bitcast.129), channel_id=1, replica_groups=mesh['row'=8,'col'=4] {'col'}, dimensions={0}, use_global_device_ids=true | all-gather | bytes 163840 | tf_op jit(solution)/shard_map/all_gather | solution.py:52
  46.8 21.7 %all-gather.3.cloned.1.call-done = bf16[128,128,32]{2,1,0:T(8,128)(2,1)} async-done(((bf16[128,16,32]{2,1,0:T(8,128)(2,1)}), bf16[128,128,32]{2,1,0:T(8,128)(2,1)}) %all-gather.3.cloned.1.call-update) | async-done | bytes 1048592 | tf_op jit(solution)/shard_map/all_gather | solution.py:56
  69.8 1.8 copy.50
  71.6 32.6 %while.17 = (s32[]{:T(128)}, f32[128,32,32]{0,2,1:T(8,128)}, f32[1024,128]{1,0:T(8,128)S(1)}, bf16[2,8,32,128]{3,2,1,0:T(8,128)(2,1)}, bf16[2,128,8,32]{1,3,2,0:...) while((s32[]{:T(128)}, f32[128,32,32]{0,2,1:T(8,128)}, ...), condition=%wide.region_3.4_spmd.clone, body=%wide.region_2.3_spmd.clone.sunk | while | flops 404193280 | bytes 15928666 | solution.py:106
  74.8 1.7 fusion.79
  76.5 2.2 reshape.96
  81.1 1.6 reshape.95
  82.7 1.5 fusion.78
  85.3 2.1 fusion.81
  90.6 1.7 fusion.79
  92.3 2.2 reshape.96
  96.9 1.6 reshape.95
  98.5 2.6 fusion.78
  102.1 2.1 fusion.81
  104.3 1.8 convert_element_type.69
  106.1 1.5 convert_reduce_fusion.1
  107.6 2.1 copy.51
  109.9 50.2 %all-reduce.4.cloned.1.call-done = bf16[128,32,32]{0,2,1:T(8,128)(2,1)} async-done(((bf16[128,32,32]{0,2,1:T(8,128)(2,1)}), bf16[128,32,32]{0,2,1:T(8,128)(2,1)}) %all-reduce.4.cloned.1.call-update) | async-done | bytes 262160 | tf_op jit(solution)/shard_map/psum | solution.py:114
  161.0 19.8 %all-gather = bf16[512,16,32]{0,2,1:T(8,128)(2,1)S(1)} all-gather(bf16[128,16,32]{0,2,1:T(8,128)(2,1)S(1)} %fusion.28), channel_id=2, replica_groups=mesh['row'=8,'col'=4] {'col'}, dimensions={0}, use_global_device_ids=true | all-gather | bytes 655360 | tf_op jit(solution)/shard_map/all_gather | solution.py:9
  182.8 2.9 reduce-scatter.4.cloned.1.call-done
  190.8 120.9 %all-reduce.6.cloned.1.call-done = (f32[256,32]{0,1:T(8,128)}, f32[256,32]{0,1:T(8,128)}, f32[256]{0:T(256)}, f32[128]{0:T(128)}) async-done(((f32[256,32]{0,1:T(8,128)}, f32[256,32]{0,1:T(8,128)}, f32[256]{0:T(256)}, f32[128]{0:T(128)}), (f32[256,32]{0,1:T(8,128)}, f32[256,32]{0,1:T(8,128)}, f32[256]{0:T(256)}, f32[128]{0:T(128)})) %all-reduce.6.cloned.1.call-update) | async-done | bytes 67088 | tf_op jit(solution)/shard_map/psum | solution.py:155
  314.4 37.1 %reduce-scatter.6.cloned.1.call-done = bf16[128,128]{1,0:T(8,128)(2,1)} async-done(((bf16[1024,128]{1,0:T(8,128)(2,1)}), bf16[128,128]{1,0:T(8,128)(2,1)}) %reduce-scatter.6.cloned.1.call-update) | async-done | bytes 32784 | tf_op jit(solution)/shard_map/reduce_scatter | solution.py:156
  354.0 18.8 %reduce-scatter.8.cloned.1.call-done = f32[32,128]{1,0:T(8,128)} async-done(((f32[128,128]{1,0:T(8,128)}), f32[32,128]{1,0:T(8,128)}) %reduce-scatter.8.cloned.1.call-update) | async-done | bytes 16400 | tf_op jit(solution)/shard_map/reduce_scatter | solution.py:159
  (106 shorter events, 30.2 us)
Async XLA Ops:
  7.2 3.6 copy-start
  7.2 22.1 %copy-start.12 = (bf16[256,32]{0,1:T(8,128)(2,1)S(1)}, bf16[256,32]{0,1:T(8,128)(2,1)}, u32[]{:S(2)}) copy-start(bf16[256,32]{0,1:T(8,128)(2,1)} %param.11) | copy-start | bytes 49156
  7.2 61.3 %all-gather.3.cloned.1.call-start = ((), (), s32[]{:S(2)}) async-start(), calls=%async_computation.3 | async-start | bytes 4718592 | tf_op jit(solution)/shard_map/all_gather | solution.py:56
  8.3 2.4 copy-start.8
  10.8 18.8 %copy-start.5 = (bf16[32,16,256]{2,1,0:T(8,128)(2,1)}, bf16[32,16,256]{2,1,0:T(8,128)(2,1)S(1)}, u32[]{:S(2)}) copy-start(bf16[32,16,256]{2,1,0:T(8,128)(2,1)S(1)} %fusion.21) | copy-start | bytes 786436
  29.1 131.0 %all-reduce.4.cloned.1.call-start = ((), (), s32[]{:S(2)}) async-start(), calls=%async_computation.5 | async-start | bytes 524288 | tf_op jit(solution)/shard_map/psum | solution.py:114
  45.9 25.7 %copy-start.1 = (bf16[1024,128]{1,0:T(8,128)(2,1)S(1)}, bf16[1024,128]{1,0:T(8,128)(2,1)}, u32[]{:S(2)}) copy-start(bf16[1024,128]{1,0:T(8,128)(2,1)} %param.13) | copy-start | bytes 786436
  82.7 1.6 copy-start.15
  82.7 1.9 copy-start.16
  84.3 3.1 copy-start.3
  98.5 2.6 copy-start.15
  98.5 2.9 copy-start.16
  101.1 3.1 copy-start.3
  106.1 79.6 %reduce-scatter.4.cloned.1.call-start = ((), (), s32[]{:S(2)}) async-start(), calls=%async_computation.4 | async-start | bytes 655360 | tf_op jit(solution)/shard_map/reduce_scatter | solution.py:111
  107.6 74.3 %copy-start.6 = (bf16[32,16,256]{2,1,0:T(8,128)(2,1)S(1)}, bf16[32,16,256]{2,1,0:T(8,128)(2,1)}, u32[]{:S(2)}) copy-start(bf16[32,16,256]{2,1,0:T(8,128)(2,1)} %copy-done.5) | copy-start | bytes 786436
  109.8 75.9 %copy-start.13 = (bf16[256,32]{0,1:T(8,128)(2,1)S(1)}, bf16[256,32]{0,1:T(8,128)(2,1)}, u32[]{:S(2)}) copy-start(bf16[256,32]{0,1:T(8,128)(2,1)} %param.11) | copy-start | bytes 49156
  109.8 77.0 %copy-start.14 = (f32[256]{0:T(256)S(1)}, f32[256]{0:T(256)}, u32[]{:S(2)}) copy-start(f32[256]{0:T(256)} %param.10) | copy-start | bytes 3076
  109.8 201.9 %all-reduce.6.cloned.1.call-start = ((), (), s32[]{:S(2)}) async-start(), calls=%async_computation.8 | async-start | bytes 134144 | tf_op jit(solution)/shard_map/psum | solution.py:155
  180.8 6.3 %copy-start.4 = (bf16[32,16,256]{2,1,0:T(8,128)(2,1)S(1)}, bf16[32,16,256]{2,1,0:T(8,128)(2,1)}, u32[]{:S(2)}) copy-start(bf16[32,16,256]{2,1,0:T(8,128)(2,1)} %param.9) | copy-start | bytes 786436
  180.8 6.3 %copy-start.9 = (f32[32,16]{1,0:T(8,128)S(1)}, f32[32,16]{1,0:T(8,128)}, u32[]{:S(2)}) copy-start(f32[32,16]{1,0:T(8,128)} %copy-done.8) | copy-start | bytes 6148
  180.8 6.3 %copy-start.11 = (f32[32,16]{1,0:T(8,128)S(1)}, f32[32,16]{1,0:T(8,128)}, u32[]{:S(2)}) copy-start(f32[32,16]{1,0:T(8,128)} %copy-done.10) | copy-start | bytes 6148
  185.6 2.3 copy-start.7
  188.8 162.7 %reduce-scatter.6.cloned.1.call-start = ((), (), s32[]{:S(2)}) async-start(), calls=%async_computation.6 | async-start | bytes 294912 | tf_op jit(solution)/shard_map/reduce_scatter | solution.py:156
  189.6 183.3 %reduce-scatter.8.cloned.1.call-start = ((), (), s32[]{:S(2)}) async-start(), calls=%async_computation.7 | async-start | bytes 81920 | tf_op jit(solution)/shard_map/reduce_scatter | solution.py:159
  (5 other events, 4.1 us)
Sparse Core Ops, SparseCore 0:
  29.3 39.2 all-gather.2
  106.2 53.8 all-reduce.3
  162.4 23.2 reduce-scatter.3
  192.2 119.4 all-reduce.5
  314.6 36.8 reduce-scatter.5
  353.5 19.2 reduce-scatter.7
